TPU v7x, 32 devices: a whole 2x2x4 slice. The times are simulated.
32 devices in a mesh: dp: 2 (over x), tp: 4 (over z), ep: 4 (over y, core).
Axes of the slice: x: 2, y: 2, z: 4, core: 2. Of those that a mesh axis runs over, the one named last changes fastest.
Arguments:
- x: bfloat16 [256, 2048], P(('dp', 'tp', 'ep')), parts along dimension 0
- kv0: bfloat16 [256, 256, 576], P(('dp', 'tp', 'ep')), parts along dimension 0
- kv1: bfloat16 [256, 256, 576], P(('dp', 'tp', 'ep')), parts along dimension 0
- lens: int32 [256], P(('dp', 'tp', 'ep')), parts along dimension 0
- ids: int32 [256, 6], P(('dp', 'tp', 'ep')), parts along dimension 0
- wts: float32 [256, 6], P(('dp', 'tp', 'ep')), parts along dimension 0
- wq: bfloat16 [2, 2048, 3072], replicated
- wuk: bfloat16 [2, 16, 128, 512], replicated
- wuv: bfloat16 [2, 16, 512, 128], replicated
- wo: bfloat16 [2, 2048, 2048], replicated
- w_in: bfloat16 [2, 2, 2048, 11264], P(None, None, None, 'tp')
- w_out: bfloat16 [2, 11264, 2048], P(None, 'tp')
- e_in: bfloat16 [64, 2048, 2816], P(('tp', 'ep'))
- e_out: bfloat16 [64, 1408, 2048], P(('tp', 'ep'))
Outputs:
- output: bfloat16 [256, 2048], P(('dp', 'tp', 'ep')), parts along dimension 0
There are 2 independent parts. A program takes and returns all parts, laid end to end along the dimension named above; an argument that names none is the same for every part.
All inputs are finite; a program needn't handle non-finite values.
Results may differ from a plain program's by a relative error of at most 0.0157094.
Values are sent between devices in bfloat16 or wider.
A program may use at most 1 GiB of HBM per device.

v0:
```python
import functools
import jax
import jax.numpy as jnp
from jax import lax
from jax.sharding import PartitionSpec as P

BATCH = ('dp', 'tp', 'ep')
GROUP = ('tp', 'ep')


def rms(v):
    vf = v.astype(jnp.float32)
    return (vf * lax.rsqrt(jnp.mean(vf * vf, axis=-1, keepdims=True) + 1e-6)).astype(jnp.bfloat16)


def rope_q(q, pos):
    half = q.shape[-1] // 2
    freq = 10000.0 ** (-2.0 * jnp.arange(half, dtype=jnp.float32) / q.shape[-1])
    ang = pos.astype(jnp.float32)[:, None, None] * freq
    cs = jnp.cos(ang)
    sn = jnp.sin(ang)
    q1 = q[..., :half]
    q2 = q[..., half:]
    return jnp.concatenate([q1 * cs - q2 * sn, q2 * cs + q1 * sn], axis=-1)


def mla(a, cache, lens, wq, wuk, wuv, wo):
    b = a.shape[0]
    heads, nope, lat = wuk.shape
    rope = cache.shape[2] - lat
    q = jnp.dot(a, wq, preferred_element_type=jnp.float32).reshape(b, heads, nope + rope)
    ql = jnp.einsum('bhn,hnl->bhl', q[..., :nope].astype(jnp.bfloat16), wuk, preferred_element_type=jnp.float32).astype(jnp.bfloat16)
    qc = jnp.concatenate([ql, rope_q(q[..., nope:], lens).astype(jnp.bfloat16)], axis=-1)
    s = jnp.einsum('cie,cle->cil', qc, cache, preferred_element_type=jnp.float32) * (nope + rope) ** -0.5
    s = jnp.where(jnp.arange(cache.shape[1])[None, None, :] < lens[:, None, None], s, -1e30)
    p = jax.nn.softmax(s, axis=-1).astype(jnp.bfloat16)
    ol = jnp.einsum('bhk,bkl->bhl', p, cache[:, :, :lat], preferred_element_type=jnp.float32).astype(jnp.bfloat16)
    o = jnp.einsum('bhl,hlv->bhv', ol, wuv, preferred_element_type=jnp.float32).astype(jnp.bfloat16)
    return jnp.dot(o.reshape(b, -1), wo, preferred_element_type=jnp.float32)


def ffn_tp(a, wi, wd):
    b = a.shape[0]
    ag = lax.all_gather(a, 'tp', axis=0, tiled=True)
    g = jnp.dot(ag, wi[0], preferred_element_type=jnp.float32)
    up = jnp.dot(ag, wi[1], preferred_element_type=jnp.float32)
    act = (jax.nn.silu(g) * up).astype(jnp.bfloat16)
    pr = jnp.dot(act, wd, preferred_element_type=jnp.float32).astype(jnp.bfloat16)
    back = lax.all_to_all(pr.reshape(-1, b, pr.shape[1]), 'tp', 0, 0)
    return jnp.sum(back.astype(jnp.float32), axis=0)


def experts_local(rows, rid, e_in, e_out):
    el = e_in.shape[0]
    eff = e_out.shape[1]
    order = jnp.argsort(rid)
    sizes = jnp.sum((rid[:, None] == jnp.arange(el)[None, :]).astype(jnp.int32), axis=0).astype(jnp.int32)
    gu = lax.ragged_dot(rows[order], e_in, sizes, preferred_element_type=jnp.float32)
    act = (jax.nn.silu(gu[:, :eff]) * gu[:, eff:]).astype(jnp.bfloat16)
    out = lax.ragged_dot(act, e_out, sizes, preferred_element_type=jnp.float32).astype(jnp.bfloat16)
    return jnp.zeros_like(rows).at[order].set(out)


def moe_ep(u, ids, wts, e_in, e_out, n):
    b, h = u.shape
    k = ids.shape[1]
    el = e_in.shape[0]
    cap = -(-(b * k) // n)
    fid = ids.reshape(-1)
    fw = wts.reshape(-1)
    isff = fid < el * n
    dst = jnp.where(isff, fid // el, n)
    oh = (dst[:, None] == jnp.arange(n)[None, :]).astype(jnp.int32)
    pos = jnp.sum((jnp.cumsum(oh, axis=0) - oh) * oh, axis=1)
    slot = jnp.where(isff, dst * cap + pos, n * cap)
    stok = jnp.zeros((n * cap,), jnp.int32).at[slot].set(jnp.arange(b * k) // k, mode='drop')
    sid = jnp.full((n * cap,), el, jnp.int32).at[slot].set(fid % el, mode='drop')
    recv = lax.all_to_all(u[stok].reshape(n, cap, h), GROUP, 0, 0)
    rid = lax.all_to_all(sid.reshape(n, cap), GROUP, 0, 0)
    out = experts_local(recv.reshape(n * cap, h), rid.reshape(-1), e_in, e_out)
    ret = lax.all_to_all(out.reshape(n, cap, h), GROUP, 0, 0).reshape(n * cap, h)
    got = ret[jnp.minimum(slot, n * cap - 1)].astype(jnp.float32)
    contrib = jnp.where(isff[:, None], fw[:, None] * got, 0.0)
    zw = jnp.sum(jnp.where(isff, 0.0, fw).reshape(b, k), axis=1)
    return jnp.sum(contrib.reshape(b, k, h), axis=1) + zw[:, None] * u.astype(jnp.float32)


def layer(x, kv0, kv1, lens, ids, wts, wq, wuk, wuv, wo, w_in, w_out, e_in, e_out, n):
    h0 = (x.astype(jnp.float32) + mla(rms(x), kv0, lens, wq[0], wuk[0], wuv[0], wo[0])).astype(jnp.bfloat16)
    u = rms(h0)
    m = moe_ep(u, ids, wts, e_in, e_out, n)
    f0 = (h0.astype(jnp.float32) + ffn_tp(u, w_in[0], w_out[0])).astype(jnp.bfloat16)
    h1 = (f0.astype(jnp.float32) + mla(rms(f0), kv1, lens, wq[1], wuk[1], wuv[1], wo[1])).astype(jnp.bfloat16)
    y = h1.astype(jnp.float32) + ffn_tp(rms(h1), w_in[1], w_out[1]) + m
    return y.astype(jnp.bfloat16)


def solution(mesh):
    n = mesh.shape['tp'] * mesh.shape['ep']
    in_specs = (P(BATCH, None), P(BATCH, None, None), P(BATCH, None, None), P(BATCH), P(BATCH, None), P(BATCH, None),
                P(), P(), P(), P(), P(None, None, None, 'tp'), P(None, 'tp', None), P(GROUP, None, None), P(GROUP, None, None))
    return jax.shard_map(functools.partial(layer, n=n), mesh=mesh, in_specs=in_specs, out_specs=P(BATCH, None), check_vma=False)
```

profile of v0, /device:TPU:0, one launch (start us, length us, event | category | flops | bytes accessed | tf_op | source)
XLA Modules:
  0.0 239.5 jit_solution(12928878264890092488)
XLA Ops:
  0.0 0.8 reshape.339
  0.8 0.8 reshape.338
  1.9 0.7 scatter_custom_fusion
  3.3 7.4 %all-to-all-start.2 = ((s32[16,1,3]{2,1,0:T(1,128)}), s32[16,1,3]{2,1,0:T(1,128)S(1)}, u32[]{:S(2)}, u32[]{:S(2)}) async-start(s32[16,1,3]{2,1,0:T(1,128)} %bitcast.30), calls=%async_computation.2 | async-start | bytes 16384 | tf_op jit(solution)/shard_map/all_to_all | solution.py:79
  11.5 0.7 iota_compare_fusion.1
  12.2 17.5 %slice_bitcast_fusion = (bf16[3072,2048]{0,1:T(8,128)(2,1)}, bf16[3072,2048]{0,1:T(8,128)(2,1)}) fusion(bf16[2,2048,3072]{2,1,0:T(8,128)(2,1)} %param.20), kind=kLoop, calls=%fused_computation.8 | loop fusion | bytes 50331648 | tf_op jit(solution)/shard_map/dot_general | solution.py:31
  29.7 16.7 %copy.36 = bf16[3072,2048]{1,0:T(8,128)(2,1)} copy(bf16[3072,2048]{0,1:T(8,128)(2,1)} %get-tuple-element.22) | data formatting | bytes 25165824 | tf_op jit(solution)/shard_map/dot_general | solution.py:31
  46.6 8.1 %fusion.160 = f32[8,16,192]{2,0,1:T(8,128)S(1)} fusion(bf16[16,192,2048]{2,1,0:T(8,128)(2,1)} %bitcast.157, bf16[8,2048]{1,0:T(8,128)(2,1)S(1)} %copy-done.4, f32[8]{0:T(128)S(1)} %add_rsqrt_fusion.3), kind=kOutput, calls=%fused_computation.135 | convolution fusion | flops 100712448 | bytes 12714016 | tf_op jit(solution)/shard_map/dot_general | solution.py:31
  56.7 5.7 %multiply_reduce_fusion.1 = (f32[8]{0:T(128)S(1)}, f32[8,2048]{1,0:T(8,128)S(1)}) fusion(bf16[2,2048,2048]{2,1,0:T(8,128)(2,1)} %param.23, bf16[2,16,512,128]{3,2,1,0:T(8,128)(2,1)} %param.22, bf16[8,16,512]{2,1,0:T(8,128)(2,1)S(1)} %fusion.84, bf16[8,2048]{1,0:T(8,128)(2,1)S(1)} %copy-done.4), kind=kOutput, calls=%fused_computation.128 | convolution fusion | flops 84000760 | bytes 10715168 | tf_op jit(solution)/shard_map/dot_general | solution.py:39
  62.4 13.8 %all_gather.6 = bf16[32,2048]{1,0:T(8,128)(2,1)S(1)} all-gather(bf16[8,2048]{1,0:T(8,128)(2,1)S(1)} %multiply_convert_fusion.1), channel_id=1, replica_groups=mesh['dp'=2,'tp'=4,'ep'=4] {'tp'}, dimensions={0}, use_global_device_ids=true | all-gather | bytes 163840 | tf_op jit(solution)/shard_map/all_gather | solution.py:44
  77.0 6.3 %fusion.12 = f32[32,2816]{1,0:T(8,128)S(1)} fusion(bf16[32,2048]{1,0:T(8,128)(2,1)S(1)} %all_gather.6, bf16[2,2,2048,2816]{3,2,1,0:T(8,128)(2,1)} %param.24), kind=kOutput, calls=%fused_computation.20 | convolution fusion | flops 369098752 | bytes 12025856 | tf_op jit(solution)/shard_map/dot_general | solution.py:45
  83.3 10.3 %fusion.47 = bf16[4,8,2048]{2,1,0:T(8,128)(2,1)} fusion(bf16[2,2816,2048]{2,1,0:T(8,128)(2,1)} %param.25, bf16[32,2048]{1,0:T(8,128)(2,1)S(1)} %all_gather.6, bf16[2,2,2048,2816]{3,2,1,0:T(8,128)(2,1)} %param.24, f32[32,2816]{1,0:T(8,128)S(1)} %fusion.12), kind=kOutput, calls=%fused_computation.41 | convolution fusion | flops 738803712 | bytes 23691264 | tf_op jit(solution)/shard_map/dot_general | solution.py:48
  93.7 16.7 %copy.40 = bf16[3072,2048]{1,0:T(8,128)(2,1)} copy(bf16[3072,2048]{0,1:T(8,128)(2,1)} %get-tuple-element.21) | data formatting | bytes 25165824 | tf_op jit(solution)/shard_map/dot_general | solution.py:31
  111.1 0.8 reshape.341
  111.9 4.6 %all-to-all-start = ((bf16[4,8,2048]{2,1,0:T(8,128)(2,1)}), bf16[4,8,2048]{2,1,0:T(8,128)(2,1)S(1)}, u32[]{:S(2)}, u32[]{:S(2)}) async-start(bf16[4,8,2048]{2,1,0:T(8,128)(2,1)} %fusion.47), calls=%async_computation | async-start | bytes 262144 | tf_op jit(solution)/shard_map/all_to_all | solution.py:49
  117.8 2.0 sort.17
  120.5 1.4 ragged-dot-metadata
  122.2 5.8 %all-to-all-start.3 = ((bf16[16,3,2048]{2,1,0:T(4,128)(2,1)}), bf16[16,3,2048]{2,1,0:T(4,128)(2,1)S(1)}, u32[]{:S(2)}, u32[]{:S(2)}) async-start(bf16[16,3,2048]{2,1,0:T(4,128)(2,1)} %reshape.341), calls=%async_computation.3 | async-start | bytes 524288 | tf_op jit(solution)/shard_map/all_to_all | solution.py:78
  128.2 8.1 %fusion.157 = f32[8,16,192]{2,0,1:T(8,128)S(1)} fusion(bf16[16,192,2048]{2,1,0:T(8,128)(2,1)} %bitcast.156, bf16[8,2048]{1,0:T(8,128)(2,1)S(1)} %get-tuple-element.18, f32[8]{0:T(128)S(1)} %add_rsqrt_fusion.1), kind=kOutput, calls=%fused_computation.133 | convolution fusion | flops 100712448 | bytes 12714016 | tf_op jit(solution)/shard_map/dot_general | solution.py:31
  138.1 5.7 %multiply_reduce_fusion = (f32[8]{0:T(128)S(1)}, f32[8,2048]{1,0:T(8,128)S(1)}) fusion(bf16[2,2048,2048]{2,1,0:T(8,128)(2,1)} %param.23, bf16[2,16,512,128]{3,2,1,0:T(8,128)(2,1)} %param.22, bf16[8,16,512]{2,1,0:T(8,128)(2,1)S(1)} %fusion.87, bf16[8,2048]{1,0:T(8,128)(2,1)S(1)} %get-tuple-element.18), kind=kOutput, calls=%fused_computation.122 | convolution fusion | flops 84000760 | bytes 10715168 | tf_op jit(solution)/shard_map/dot_general | solution.py:39
  143.9 13.8 %all_gather.7 = bf16[32,2048]{1,0:T(8,128)(2,1)S(1)} all-gather(bf16[8,2048]{1,0:T(8,128)(2,1)S(1)} %multiply_convert_fusion), channel_id=1, replica_groups=mesh['dp'=2,'tp'=4,'ep'=4] {'tp'}, dimensions={0}, use_global_device_ids=true | all-gather | bytes 163840 | tf_op jit(solution)/shard_map/all_gather | solution.py:44
  157.7 6.3 %fusion.6 = f32[32,2816]{1,0:T(8,128)S(1)} fusion(bf16[32,2048]{1,0:T(8,128)(2,1)S(1)} %all_gather.7, bf16[2,2,2048,2816]{3,2,1,0:T(8,128)(2,1)} %param.24), kind=kOutput, calls=%fused_computation.14 | convolution fusion | flops 369098752 | bytes 12025856 | tf_op jit(solution)/shard_map/dot_general | solution.py:45
  164.0 10.3 %fusion.44 = bf16[4,8,2048]{2,1,0:T(8,128)(2,1)} fusion(bf16[2,2816,2048]{2,1,0:T(8,128)(2,1)} %param.25, bf16[32,2048]{1,0:T(8,128)(2,1)S(1)} %all_gather.7, bf16[2,2,2048,2816]{3,2,1,0:T(8,128)(2,1)} %param.24, f32[32,2816]{1,0:T(8,128)S(1)} %fusion.6), kind=kOutput, calls=%fused_computation.40 | convolution fusion | flops 738803712 | bytes 23691264 | tf_op jit(solution)/shard_map/dot_general | solution.py:48
  174.3 4.6 %all-to-all-start.1 = ((bf16[4,8,2048]{2,1,0:T(8,128)(2,1)}), bf16[4,8,2048]{2,1,0:T(8,128)(2,1)S(1)}, u32[]{:S(2)}, u32[]{:S(2)}) async-start(bf16[4,8,2048]{2,1,0:T(8,128)(2,1)} %fusion.44), calls=%async_computation.1 | async-start | bytes 262144 | tf_op jit(solution)/shard_map/all_to_all | solution.py:49
  179.1 1.4 gather_fusion.1
  180.5 23.9 %ragged-dot-none.1 = f32[48,2816]{1,0:T(8,128)} custom-call(s32[1]{0:T(128)} %get-tuple-element.7, s32[5]{0:T(128)} %get-tuple-element.8, s32[6]{0:T(128)} %get-tuple-element.9, s32[6]{0:T(128)} %get-tuple-element.10, s32[1]{0:T(128)} %get-tuple-element.7, bf16[48,2048]{1,0:T(8,128)(2,1)} %gather_fusion.1, bf16[4,2048,2816]{2,1,0:T(8,128)(2,1)} %param.26), custom_call_target="tpu_custom_call" | custom-call | flops 553648128 | bytes 46874640 | tf_op jit(solution)/shard_map/ragged_dot_general/ragged-dot-none
  204.4 1.8 fusion.138
  206.2 15.1 %ragged-dot-none = f32[48,2048]{1,0:T(8,128)} custom-call(s32[1]{0:T(128)} %get-tuple-element.7, s32[5]{0:T(128)} %get-tuple-element.8, s32[6]{0:T(128)} %get-tuple-element.9, s32[6]{0:T(128)} %get-tuple-element.10, s32[1]{0:T(128)} %get-tuple-element.7, bf16[48,1408]{1,0:T(8,128)(2,1)} %fusion.138, bf16[4,1408,2048]{2,1,0:T(8,128)(2,1)} %param.27), custom_call_target="tpu_custom_call" | custom-call | flops 276824064 | bytes 23597072 | tf_op jit(solution)/shard_map/ragged_dot_general/ragged-dot-none
  221.4 1.4 scatter_custom_fusion.2
  222.8 0.8 reshape.343
  223.6 4.2 %all-to-all-start.4 = ((bf16[16,3,2048]{2,1,0:T(4,128)(2,1)}), bf16[16,3,2048]{2,1,0:T(4,128)(2,1)S(1)}, u32[]{:S(2)}, u32[]{:S(2)}) async-start(bf16[16,3,2048]{2,1,0:T(4,128)(2,1)} %reshape.343), calls=%async_computation.4 | async-start | bytes 524288 | tf_op jit(solution)/shard_map/all_to_all | solution.py:81
  228.0 9.6 %all-to-all-done.4 = bf16[16,3,2048]{2,1,0:T(4,128)(2,1)S(1)} async-done(((bf16[16,3,2048]{2,1,0:T(4,128)(2,1)}), bf16[16,3,2048]{2,1,0:T(4,128)(2,1)S(1)}, u32[]{:S(2)}, u32[]{:S(2)}) %all-to-all-start.4) | async-done | bytes 196640 | tf_op jit(solution)/shard_map/all_to_all | solution.py:81
  (70 shorter events, 11.9 us)
Async XLA Ops:
  3.3 108.6 %all-to-all-start.2 = ((s32[16,1,3]{2,1,0:T(1,128)}), s32[16,1,3]{2,1,0:T(1,128)S(1)}, u32[]{:S(2)}, u32[]{:S(2)}) async-start(s32[16,1,3]{2,1,0:T(1,128)} %bitcast.30), calls=%async_computation.2 | async-start | bytes 16384 | tf_op jit(solution)/shard_map/all_to_all | solution.py:79
  29.7 16.7 %copy-start.4 = (bf16[8,2048]{1,0:T(8,128)(2,1)S(1)}, bf16[8,2048]{1,0:T(8,128)(2,1)}, u32[]{:S(2)}) copy-start(bf16[8,2048]{1,0:T(8,128)(2,1)} %param.14) | copy-start | bytes 98308
  46.5 8.4 %copy-start = (bf16[2,16,128,512]{3,2,1,0:T(8,128)(2,1)S(1)}, bf16[2,16,128,512]{3,2,1,0:T(8,128)(2,1)}, u32[]{:S(2)}) copy-start(bf16[2,16,128,512]{3,2,1,0:T(8,128)(2,1)} %param.21) | copy-start | bytes 12582916
  46.5 8.9 %copy-start.2 = (bf16[8,256,576]{1,2,0:T(8,128)(2,1)S(1)}, bf16[8,256,576]{1,2,0:T(8,128)(2,1)}, u32[]{:S(2)}) copy-start(bf16[8,256,576]{1,2,0:T(8,128)(2,1)} %param.15) | copy-start | bytes 7077892
  110.4 26.5 %copy-start.3 = (bf16[8,256,576]{1,2,0:T(8,128)(2,1)S(1)}, bf16[8,256,576]{1,2,0:T(8,128)(2,1)}, u32[]{:S(2)}) copy-start(bf16[8,256,576]{1,2,0:T(8,128)(2,1)} %param.16) | copy-start | bytes 7077892
  111.9 10.3 %all-to-all-start = ((bf16[4,8,2048]{2,1,0:T(8,128)(2,1)}), bf16[4,8,2048]{2,1,0:T(8,128)(2,1)S(1)}, u32[]{:S(2)}, u32[]{:S(2)}) async-start(bf16[4,8,2048]{2,1,0:T(8,128)(2,1)} %fusion.47), calls=%async_computation | async-start | bytes 262144 | tf_op jit(solution)/shard_map/all_to_all | solution.py:49
  122.2 52.1 %all-to-all-start.3 = ((bf16[16,3,2048]{2,1,0:T(4,128)(2,1)}), bf16[16,3,2048]{2,1,0:T(4,128)(2,1)S(1)}, u32[]{:S(2)}, u32[]{:S(2)}) async-start(bf16[16,3,2048]{2,1,0:T(4,128)(2,1)} %reshape.341), calls=%async_computation.3 | async-start | bytes 524288 | tf_op jit(solution)/shard_map/all_to_all | solution.py:78
  128.0 8.3 %copy-start.1 = (bf16[2,16,128,512]{3,2,1,0:T(8,128)(2,1)S(1)}, bf16[2,16,128,512]{3,2,1,0:T(8,128)(2,1)}, u32[]{:S(2)}) copy-start(bf16[2,16,128,512]{3,2,1,0:T(8,128)(2,1)} %param.21) | copy-start | bytes 12582916
  174.3 49.3 %all-to-all-start.1 = ((bf16[4,8,2048]{2,1,0:T(8,128)(2,1)}), bf16[4,8,2048]{2,1,0:T(8,128)(2,1)S(1)}, u32[]{:S(2)}, u32[]{:S(2)}) async-start(bf16[4,8,2048]{2,1,0:T(8,128)(2,1)} %fusion.44), calls=%async_computation.1 | async-start | bytes 262144 | tf_op jit(solution)/shard_map/all_to_all | solution.py:49
  206.2 21.6 %copy-start.5 = (s32[8,6]{1,0:T(8,128)S(1)}, s32[8,6]{1,0:T(8,128)}, u32[]{:S(2)}) copy-start(s32[8,6]{1,0:T(8,128)} %param.18) | copy-start | bytes 580
  206.2 21.6 %copy-start.6 = (f32[8,6]{1,0:T(8,128)S(1)}, f32[8,6]{1,0:T(8,128)}, u32[]{:S(2)}) copy-start(f32[8,6]{1,0:T(8,128)} %param.19) | copy-start | bytes 580
  223.6 14.0 %all-to-all-start.4 = ((bf16[16,3,2048]{2,1,0:T(4,128)(2,1)}), bf16[16,3,2048]{2,1,0:T(4,128)(2,1)S(1)}, u32[]{:S(2)}, u32[]{:S(2)}) async-start(bf16[16,3,2048]{2,1,0:T(4,128)(2,1)} %reshape.343), calls=%async_computation.4 | async-start | bytes 524288 | tf_op jit(solution)/shard_map/all_to_all | solution.py:81
where the time goes:
time: 242 us; the launch traced here: 240 us
  matrix products  63.7 us (26%)
  local copies, waits for them, and re-layouts  60 us (25%)
  Pallas kernels  40.5 us (17%)
  blocking collectives  27.6 us (11%)
  starting transfers between devices  26.7 us (11%)
  other arithmetic  10.7 us (4%)
  waiting for transfers between devices  10 us (4%)
    dot_general x3, local copies, waits for them, and re-layouts, mla(): jnp.dot(a, wq, preferred_element_type=jnp.float32)  50.9 us
    another operation x2, Pallas kernels  39.1 us
    all_gather x2, blocking collectives, ffn_tp(): ag = lax.all_gather(a, 'tp', axis=0, tiled=True)  27.6 us
    dot_general x2, matrix products, ffn_tp(): jnp.dot(act, wd, preferred_element_type=jnp.float32).astype(jnp.bfloat16)  20.7 us
    dot_general x2, matrix products, mla(): jnp.dot(a, wq, preferred_element_type=jnp.float32)  16.2 us
    dot_general x2, matrix products, ffn_tp(): g = jnp.dot(ag, wi[0], preferred_element_type=jnp.float32)  12.6 us
    dot_general x2, matrix products, mla(): return jnp.dot(o.reshape(b, -1), wo, preferred_element_type=jnp.float32)  11.3 us
    all_to_all x1, waiting for transfers between devices, moe_ep(): lax.all_to_all(out.reshape(n, cap, h), GROUP, 0, 0).reshape(n * cap, h)  9.63 us
  transfers between devices with their start and end apart: 5, of which 2 were waited for; matrix products, arithmetic and copies ran while one was open for 54% of the time, Pallas kernels for 17%

commit v1 on v0

v1 whole, which is shorter than its diff:
```python
import functools
import types

import jax
import jax.numpy as jnp
import numpy as np
from jax import lax
from jax.experimental import pallas as pl
from jax.experimental.pallas import tpu as pltpu
from jax.sharding import PartitionSpec as P

BATCH = ('dp', 'tp', 'ep')
GROUP = ('tp', 'ep')
MESH = pl.DeviceIdType.MESH
BF = jnp.bfloat16
F32 = jnp.float32
I32 = jnp.int32

B = 8
H = 2048
HEADS = 16
NOPE = 128
ROPE = 64
LAT = 512
VH = 128
L = 256
FH = 1408
TP = 4
N = 16
R = HEADS * B
M = 64
CB = 512
SCALE = (NOPE + ROPE) ** -0.5

ALONG = (1, 3, 2)


def scratch():
    dma = pltpu.SemaphoreType.DMA
    v = pltpu.VMEM
    return dict(
        mbuf=v((8, H, CB), BF), wukb=v((HEADS, NOPE, LAT), BF), wuvb=v((HEADS, LAT, VH), BF), kvb=v((B * L, LAT + ROPE), BF),
        gu5=v((2, 5, H, CB), BF), gu1=v((2, H, CB // 2), BF), wd=v((2, 4, FH, CB), BF),
        qs=v((B, HEADS * (NOPE + ROPE)), F32), qc=v((R, LAT + ROPE), BF), sc=v((R, L), F32), pb=v((R, B * L), BF),
        ol=v((R, LAT), F32), os=v((B, HEADS * VH), BF), res=v((B, H), F32), an=v((B, H), BF),
        h0=v((B, H), BF), f0=v((B, H), BF), h1=v((B, H), BF),
        cs=v((R, ROPE), F32), sn=v((R, ROPE), F32), lm=v((R, L), F32),
        uall=v((N, B, H), BF), vall=v((N // 2, B, H), BF), fa=v((M, H), BF), ea=v((M, H), BF), act=v((M, FH), BF),
        pm=v((4, M // 2, CB), F32), ps=v((2, 4, M // 2, CB), F32), pr=v((2, 4, M // 2, CB), F32),
        bs=v((2, TP, B, H), BF), br=v((2, TP, B, H), BF),
        idall=v((N, B, 128), I32), ptk=v((N * B, M), BF), el=v((M, 128), F32), gsel=v((2 * 6 * B, 128), BF),
        racc=v((M, H), F32), rs=v((N, B, H // 2), BF), rr=v((N, B, H // 2), BF), rk=v((N * B, H // 2), BF), mm=v((B, H), F32),
        s_m=dma((8,)), s_kv=dma((B,)), s_uk=dma((2,)), s_gu=dma((2, 6, 2)), s_wd=dma((2, 4)),
        us=dma((16,)), ur=dma((N,)), vs=dma((8,)), vr=dma((N // 2,)),
        pss=dma((2, 4)), psr=dma((2, 4)), bss=dma((2, TP)), bsr=dma((2, TP)),
        ids_s=dma((N,)), ids_r=dma((N,)), ret_s=dma((N,)), ret_r=dma((N,)),
    )


def rms(v):
    vf = v.astype(F32)
    return (vf * lax.rsqrt(jnp.mean(vf * vf, axis=-1, keepdims=True) + 1e-6)).astype(BF)


def dot(a, b):
    return jnp.dot(a, b, preferred_element_type=F32)


def kernel(names, x, lens, ids, wts, table, kv0, kv1, wq, wuk, wuv, wo, w_in, w_out, e_in, e_out, y, *scr):
    s = types.SimpleNamespace(**dict(zip(names, scr)))
    z = lax.axis_index('tp')
    e = lax.axis_index('ep')
    me = z * 4 + e
    c = lax.rem(e, 2)
    pe = e + 1 - 2 * c
    ye = lax.rem(e + 2, 4)
    ype = lax.rem(pe + 2, 4)
    kvs = (kv0, kv1)
    sends = []

    barrier = pltpu.get_barrier_semaphore()
    others = []
    for i in range(1, N):
        zz, ee = lax.rem(z + i // 4, 4), lax.rem(e + i % 4, 4)
        others.append((i, zz * 4 + ee, zz, ee))
    for i, g, zz, ee in others:
        pl.semaphore_signal(barrier, inc=1, device_id=(lax.axis_index('dp'), zz, ee), device_id_type=MESH)

    def cp(src, dst, sem):
        return pltpu.make_async_copy(src, dst, sem)

    def m_q(l, j):
        k = 2 * l + j
        return cp(wq.at[l, :, pl.ds(j * CB, CB)], s.mbuf.at[k], s.s_m.at[k])

    def m_o(l, j):
        k = lax.rem(2 * l + 6 + j, 8)
        return cp(wo.at[l, :, pl.ds(j * CB, CB)], s.mbuf.at[k], s.s_m.at[k])

    def c_kv(l, t):
        return cp(kvs[l].at[t], s.kvb.at[pl.ds(t * L, L)], s.s_kv.at[t])

    def c_uk(l):
        return cp(wuk.at[l], s.wukb, s.s_uk.at[0])

    def c_uv(l):
        return cp(wuv.at[l], s.wuvb, s.s_uk.at[1])

    def u_gu(what, i, k, j, w, half):
        o = pl.multiple_of(j * 256, 128)
        if what == 'ffn':
            src = w_in.at[i, half, :, pl.ds(pl.multiple_of(c * FH + o, 128), w)]
        else:
            src = e_in.at[i, :, pl.ds(pl.multiple_of(half * FH + o, 128), w)]
        dst = s.gu5.at[k, j, :, pl.ds(half * w, w)] if w == 256 else s.gu1.at[k, :, pl.ds(half * w, w)]
        return cp(src, dst, s.s_gu.at[k, j, half])

    def u_wd(what, i, k, j):
        cols = pl.ds(pl.multiple_of(j * CB, CB), CB)
        if what == 'ffn':
            src = w_out.at[i, pl.ds(pl.multiple_of(c * FH, 128), FH), cols]
        else:
            src = e_out.at[i, :, cols]
        return cp(src, s.wd.at[k, j], s.s_wd.at[k, j])

    def u_start(what, i, k):
        def gu(j, _):
            u_gu(what, i, k, j, 256, 0).start()
            u_gu(what, i, k, j, 256, 1).start()
            return 0

        lax.fori_loop(0, 5, gu, 0)
        u_gu(what, i, k, 5, 128, 0).start()
        u_gu(what, i, k, 5, 128, 1).start()

        def dn(j, _):
            u_wd(what, i, k, j).start()
            return 0

        lax.fori_loop(0, 4, dn, 0)

    def rc(src, dst, ss, rs, tp, ep):
        return pltpu.make_async_remote_copy(src_ref=src, dst_ref=dst, send_sem=ss, recv_sem=rs,
                                            device_id=(lax.axis_index('dp'), tp, ep), device_id_type=MESH)

    def send(*a):
        d = rc(*a)
        d.start()
        sends.append(d)

    for j in range(6):
        m_q(0, j).start()
    for t in range(B):
        c_kv(0, t).start()
    c_uk(0).start()
    c_uv(0).start()
    m_o(0, 0).start()
    m_o(0, 1).start()

    diag = lax.broadcasted_iota(I32, (B, B), 0) == lax.broadcasted_iota(I32, (B, B), 1)
    lrow = jnp.broadcast_to(lens[...].astype(F32).reshape(1, B), (B, B))
    lv = jnp.broadcast_to(jnp.sum(jnp.where(diag, lrow, 0.0), axis=1, keepdims=True), (B, L))
    at = jnp.where(lax.broadcasted_iota(I32, (B, L), 1).astype(F32) == lv - 1.0, 1.0, 0.0).astype(BF)
    tb = dot(at, table[...])
    tb = tb[:, :128] + tb[:, 128:256] + tb[:, 256:]
    s.cs[...] = jnp.concatenate([tb[:, :ROPE]] * HEADS, axis=0)
    s.sn[...] = jnp.concatenate([tb[:, ROPE:]] * HEADS, axis=0)
    rowt = lax.broadcasted_iota(I32, (R, L), 0) & (B - 1)
    s.lm[...] = jnp.concatenate([lv] * HEADS, axis=0)

    def q_steps(l, lo, hi):
        def step(j, _):
            m_q(l, j).wait()
            s.qs[:, pl.ds(pl.multiple_of(j * CB, CB), CB)] = dot(s.an[...], s.mbuf[2 * l + j])
            return 0

        lax.fori_loop(lo, hi, step, 0)

    def mla(l, after_two, after_q, after_uk, after_kv, after_uv):
        q_steps(l, 0, 2)
        after_two()
        q_steps(l, 2, 6)
        after_q()
        c_uk(l).wait()
        D = NOPE + ROPE
        rope = []
        for hp in range(HEADS // 2):
            pair = []
            for k in range(2):
                h = 2 * hp + k
                qn = s.qs[:, h * D:h * D + NOPE].astype(BF)
                pair.append(dot(qn, s.wukb[h]))
                rope.append(s.qs[:, h * D + NOPE:(h + 1) * D])
            s.qc[hp * 16:(hp + 1) * 16, :LAT] = jnp.concatenate(pair, axis=0).astype(BF)
        after_uk()
        r = jnp.concatenate(rope, axis=0)
        rot = jnp.concatenate([r[:, ROPE // 2:], r[:, :ROPE // 2]], axis=1)
        s.qc[:, LAT:] = (r * s.cs[...] + rot * s.sn[...]).astype(BF)
        for t in range(B):
            c_kv(l, t).wait()
            st = lax.dot_general(s.qc[...], s.kvb[t * L:(t + 1) * L, :], (((1,), (1,)), ((), ())), preferred_element_type=F32)
            if t == 0:
                s.sc[...] = st
            else:
                s.sc[...] = jnp.where(rowt == t, st, s.sc[...])
        sc = jnp.where(lax.broadcasted_iota(I32, (R, L), 1).astype(F32) < s.lm[...], s.sc[...] * SCALE, -1e30)
        ex = jnp.exp(sc - jnp.max(sc, axis=-1, keepdims=True))
        p = ex / jnp.sum(ex, axis=-1, keepdims=True)
        for t in range(B):
            s.pb[:, t * L:(t + 1) * L] = jnp.where(rowt == t, p, 0.0).astype(BF)
        s.ol[...] = dot(s.pb[...], s.kvb[:, :LAT])
        after_kv()
        c_uv(l).wait()
        for h in range(HEADS):
            o = dot(s.ol[h * B:(h + 1) * B, :].astype(BF), s.wuvb[h])
            s.os[:, h * VH:(h + 1) * VH] = o.astype(BF)
        after_uv()

        def step(j, _):
            m_o(l, j).wait()
            s.res[:, pl.ds(pl.multiple_of(j * CB, CB), CB)] = dot(s.os[...], s.mbuf[lax.rem(2 * l + 6 + j, 8)])
            return 0

        lax.fori_loop(0, 4, step, 0)

    def unit(what, i, k, lhs, down):
        def silu(g, u):
            return (g / (1.0 + jnp.exp(-g)) * u).astype(BF)

        def gu(j, _):
            u_gu(what, i, k, j, 256, 0).wait()
            u_gu(what, i, k, j, 256, 1).wait()
            r = dot(lhs[...], s.gu5[k, j])
            s.act[:, pl.ds(pl.multiple_of(j * 256, 256), 256)] = silu(r[:, :256], r[:, 256:])
            return 0

        lax.fori_loop(0, 5, gu, 0)
        u_gu(what, i, k, 5, 128, 0).wait()
        u_gu(what, i, k, 5, 128, 1).wait()
        r = dot(lhs[...], s.gu1[k])
        s.act[:, 1280:] = silu(r[:, :128], r[:, 128:])

        def dn(j, _):
            u_wd(what, i, k, j).wait()
            down(j, dot(s.act[...], s.wd[k, j]))
            return 0

        lax.fori_loop(0, 4, dn, 0)

    def gather(buf, ss, rs, at, on_y):
        own = at(z, e)
        for k in ALONG:
            send(buf.at[own], buf.at[own], ss.at[k - 1], rs.at[own], lax.rem(z + k, TP), e)
        send(buf.at[own], buf.at[own], ss.at[3], rs.at[own], z, pe)
        if on_y:
            send(buf.at[own], buf.at[own], ss.at[8], rs.at[own], z, ye)
        for k in ALONG:
            g = at(lax.rem(z + k, TP), e)
            rc(buf.at[g], buf.at[g], ss.at[3 + k], rs.at[g], z, pe).wait_recv()
            send(buf.at[g], buf.at[g], ss.at[3 + k], rs.at[g], z, pe)
            if on_y:
                send(buf.at[g], buf.at[g], ss.at[8 + k], rs.at[g], z, ye)
        for zz in range(TP):
            g = at(zz, pe)
            rc(buf.at[g], buf.at[g], ss.at[0], rs.at[g], z, pe).wait_recv()

    def stack(buf, at):
        for i, ee in enumerate((e, pe)):
            for q in range(2):
                s.fa[i * 32 + q * 16:i * 32 + q * 16 + 16, :] = jnp.concatenate([buf[at(2 * q, ee)], buf[at(2 * q + 1, ee)]], axis=0)

    def ffn(l, k):
        def down(j, r):
            s.pm[j] = r[:M // 2]
            s.ps[l, j] = r[M // 2:]
            rc(s.ps.at[l, j], s.pr.at[l, j], s.pss.at[l, j], s.psr.at[l, j], z, pe).start()

        unit('ffn', l, k, s.fa, down)

    def ffn_send(l):
        for j in range(4):
            rc(s.ps.at[l, j], s.pr.at[l, j], s.pss.at[l, j], s.psr.at[l, j], z, pe).wait()
            tot = s.pm[j] + s.pr[l, j]
            for q in range(TP):
                s.bs[l, q, :, j * CB:(j + 1) * CB] = tot[q * B:(q + 1) * B].astype(BF)
        for k in ALONG:
            zz = lax.rem(z + k, TP)
            send(s.bs.at[l, zz], s.br.at[l, z], s.bss.at[l, k], s.bsr.at[l, z], zz, e)
        s.br[l, z] = s.bs[l, z]

    def ffn_recv(l):
        for k in ALONG:
            zz = lax.rem(z + k, TP)
            rc(s.bs.at[l, zz], s.br.at[l, zz], s.bss.at[l, k], s.bsr.at[l, zz], zz, e).wait_recv()
        acc = s.br[l, 0].astype(F32)
        for q in range(1, TP):
            acc = acc + s.br[l, q].astype(F32)
        return acc

    def at16(zz, ee):
        return zz * 4 + ee

    def at8(zz, ee):
        return zz * 2 + lax.rem(ee, 2)

    def send_ids():
        s.idall[me] = jnp.full((B, 128), -1, I32)
        s.idall[me, :, 0:6] = ids[...]
        pl.semaphore_wait(barrier, N - 1)
        for i, g, zz, ee in others:
            send(s.idall.at[me], s.idall.at[me], s.ids_s.at[i], s.ids_r.at[me], zz, ee)

    def slots_here():
        lane = lax.broadcasted_iota(I32, (B, 128), 1)
        mine = s.idall[me]
        dst = [jnp.broadcast_to(mine[:, j:j + 1], (B, 128)) >> 2 for j in range(6)]
        hot = [jnp.where(d == lane, 1.0, 0.0) for d in dst]
        cnt = functools.reduce(jnp.add, hot)
        row = lax.broadcasted_iota(I32, (B, 128), 0)
        run = jnp.zeros((B, 128), F32)
        for t in range(B - 1):
            run = run + jnp.where(row > t, jnp.broadcast_to(cnt[t:t + 1], (B, 128)), 0.0)
        left, right = [], []
        for j in range(6):
            pos = jnp.sum(hot[j] * run, axis=1, keepdims=True)
            run = run + hot[j]
            col = dst[j].astype(F32) * B + pos
            left.append(jnp.where(col == lane.astype(F32), 1.0, 0.0))
            right.append(jnp.where(col + 4.0 == lane.astype(F32), 1.0, 0.0))
        s.gsel[...] = jnp.concatenate(left + right, axis=0).astype(BF)

    def slots_there():
        for i, g, zz, ee in others:
            rc(s.idall.at[g], s.idall.at[g], s.ids_s.at[i], s.ids_r.at[g], z, pe).wait_recv()
        T = N * B
        idt = jnp.concatenate([s.idall[d] for d in range(N)], axis=0)
        lane = lax.broadcasted_iota(I32, (T, 128), 1)
        tok = lax.broadcasted_iota(I32, (T, 128), 0)
        col = [jnp.broadcast_to(idt[:, j:j + 1], (T, 128)) for j in range(6)]
        hit = [jnp.where((v >> 2) == me, 1.0, 0.0) for v in col]
        before = jnp.where((tok >> 3 == lane >> 3) & (lane < tok), 1.0, 0.0)
        run = dot(before.astype(BF), functools.reduce(jnp.add, hit).astype(BF)) + ((tok >> 3) * 4).astype(F32)
        pt = jnp.zeros((T, 128), F32)
        ex = jnp.zeros((T, 128), F32)
        for j in range(6):
            at = jnp.where(run == lane.astype(F32), hit[j], 0.0)
            pt = pt + at
            ex = ex + at * (col[j] & 3).astype(F32)
            run = run + hit[j]
        s.ptk[...] = pt[:, :M].astype(BF)
        s.el[...] = lax.dot_general(ex[:, :M].astype(BF), jnp.ones((T, 128), BF), (((0,), (0,)), ((), ())),
                                    preferred_element_type=F32)

    def expert(i, k):
        def down(j, r):
            cols = pl.ds(pl.multiple_of(j * CB, CB), CB)
            r = r.astype(BF).astype(F32)
            if i == 0:
                s.racc[:, cols] = r
            else:
                keep = jnp.broadcast_to(s.el[:, 0:1], (M, CB)) == float(i)
                s.racc[:, cols] = jnp.where(keep, r, s.racc[:, cols])

        unit('moe', i, k, s.ea, down)

    def give_back():
        for d in range(N):
            a = s.racc[4 * d:4 * d + 4, :]
            s.rs[d] = jnp.concatenate([a[:, :H // 2], a[:, H // 2:]], axis=0).astype(BF)
        for i, g, zz, ee in others:
            send(s.rs.at[g], s.rr.at[me], s.ret_s.at[i], s.ret_r.at[me], zz, ee)
        s.rr[me] = s.rs[me]

    def take_back():
        for i, g, zz, ee in others:
            rc(s.rs.at[g], s.rr.at[g], s.ret_s.at[i], s.ret_r.at[g], z, pe).wait_recv()
        for d in range(N // 2):
            s.rk[d * 16:(d + 1) * 16, :] = jnp.concatenate([s.rr[2 * d], s.rr[2 * d + 1]], axis=0)
        got = dot(s.gsel[...], s.rk[...])
        for half in range(2):
            acc = None
            for j in range(6):
                o = (half * 6 + j) * B
                term = wts[:, j:j + 1] * got[o:o + B]
                acc = term if acc is None else acc + term
            s.mm[:, half * (H // 2):(half + 1) * (H // 2)] = acc

    nothing = lambda: None

    s.an[...] = rms(x[...])

    def two0():
        m_o(0, 2).start()
        m_o(0, 3).start()
        u_start('ffn', 0, 0)
        u_start('moe', 0, 1)
        send_ids()

    def q0():
        for j in range(4):
            m_q(1, j).start()

    def kv0_done():
        for t in range(B):
            c_kv(1, t).start()

    mla(0, two0, q0, lambda: c_uk(1).start(), kv0_done, lambda: c_uv(1).start())
    for j in (4, 5):
        m_q(1, j).start()
    for j in (0, 1):
        m_o(1, j).start()
    h0 = (x[...].astype(F32) + s.res[...]).astype(BF)
    s.h0[...] = h0
    s.uall[me] = rms(h0)
    slots_here()
    gather(s.uall, s.us, s.ur, at16, True)
    slots_there()
    stack(s.uall, at16)
    ffn(0, 0)
    u_start('moe', 1, 0)
    for zz in range(TP):
        g = at16(zz, ye)
        rc(s.uall.at[g], s.uall.at[g], s.us.at[12 + zz], s.ur.at[g], z, pe).wait_recv()
        send(s.uall.at[g], s.uall.at[g], s.us.at[12 + zz], s.ur.at[g], z, pe)
    ffn_send(0)
    for zz in range(TP):
        g = at16(zz, ype)
        rc(s.uall.at[g], s.uall.at[g], s.us.at[12 + zz], s.ur.at[g], z, pe).wait_recv()
    for half in range(2):
        cols = pl.ds(half * (H // 2), H // 2)
        for d in range(N // 2):
            s.rk[d * 16:(d + 1) * 16, :] = jnp.concatenate([s.uall[2 * d, :, cols], s.uall[2 * d + 1, :, cols]], axis=0)
        s.ea[:, cols] = lax.dot_general(s.ptk[...], s.rk[...], (((0,), (0,)), ((), ())),
                                        preferred_element_type=F32).astype(BF)
    expert(0, 1)
    u_start('moe', 2, 1)
    f0 = (s.h0[...].astype(F32) + ffn_recv(0)).astype(BF)
    s.f0[...] = f0
    s.an[...] = rms(f0)

    def q1():
        m_o(1, 2).start()
        m_o(1, 3).start()

    mla(1, nothing, q1, nothing, nothing, nothing)
    h1 = (s.f0[...].astype(F32) + s.res[...]).astype(BF)
    s.h1[...] = h1
    s.vall[at8(z, e)] = rms(h1)
    gather(s.vall, s.vs, s.vr, at8, False)
    stack(s.vall, at8)
    expert(1, 0)
    u_start('moe', 3, 0)
    expert(2, 1)
    u_start('ffn', 1, 1)
    expert(3, 0)
    give_back()
    ffn(1, 1)
    ffn_send(1)
    take_back()
    y[...] = (s.h1[...].astype(F32) + ffn_recv(1) + s.mm[...]).astype(BF)
    for d in sends:
        d.wait_send()


def rope_table():
    half = ROPE // 2
    f = np.float32(10000.0) ** (np.float32(-2.0) * np.arange(half, dtype=np.float32) / np.float32(ROPE))
    ang = np.arange(1, L + 1, dtype=np.float32)[:, None] * f.astype(np.float32)
    cs, sn = np.cos(ang.astype(np.float64)), np.sin(ang.astype(np.float64))
    left = np.concatenate([cs, cs, -sn, sn], axis=1).astype(np.float32)
    parts = []
    for _ in range(3):
        part = left.astype(jnp.bfloat16)
        parts.append(part)
        left = left - part.astype(np.float32)
    return jnp.asarray(np.concatenate(parts, axis=1))


def layer(x, kv0, kv1, lens, ids, wts, wq, wuk, wuv, wo, w_in, w_out, e_in, e_out):
    table = rope_table()
    sc = scratch()
    vm = pl.BlockSpec(memory_space=pltpu.VMEM)
    hbm = pl.BlockSpec(memory_space=pl.ANY)
    return pl.pallas_call(
        functools.partial(kernel, tuple(sc)),
        out_shape=jax.ShapeDtypeStruct((B, H), BF),
        in_specs=[vm] * 5 + [hbm] * 10,
        out_specs=vm,
        scratch_shapes=list(sc.values()),
        compiler_params=pltpu.CompilerParams(collective_id=0, has_side_effects=True, vmem_limit_bytes=67043328),
    )(x, lens, ids, wts, table, kv0, kv1, wq, wuk, wuv, wo, w_in, w_out, e_in, e_out)


def solution(mesh):
    in_specs = (P(BATCH, None), P(BATCH, None, None), P(BATCH, None, None), P(BATCH), P(BATCH, None), P(BATCH, None),
                P(), P(), P(), P(), P(None, None, None, 'tp'), P(None, 'tp', None), P(GROUP, None, None), P(GROUP, None, None))
    return jax.shard_map(layer, mesh=mesh, in_specs=in_specs, out_specs=P(BATCH, None), check_vma=False)
```

time: 242 us -> 84.3 us (0.35)
  matrix products: 63.7 us -> 0 us
  local copies, waits for them, and re-layouts: 60 us -> 10.1 us
  Pallas kernels: 40.5 us -> 73.8 us
  blocking collectives: 27.6 us -> 0 us
  starting transfers between devices: 26.7 us -> 0 us
  other arithmetic: 10.7 us -> 0 us
  waiting for transfers between devices: 10 us -> 0 us
    pallas_call x0 -> x1, Pallas kernels: none -> 73.8 us  [layer(): pl.pallas_call(functools.partial(kernel, tuple(sc)), out_shape=jax.ShapeD...]
    dot_general x14 -> x0, matrix products: 63.7 us -> none  [the longest x2 20.7 us: ffn_tp(): jnp.dot(act, wd, preferred_element_type=jnp.float32).astype(jnp.bfloat16)]
    dot_general x3 -> x0, local copies, waits for them, and re-layouts: 50.9 us -> none  [mla(): jnp.dot(a, wq, preferred_element_type=jnp.float32)]
    another operation x2 -> x0, Pallas kernels: 39.1 us -> none
    all_gather x2 -> x0, blocking collectives: 27.6 us -> none  [ffn_tp(): ag = lax.all_gather(a, 'tp', axis=0, tiled=True)]
    all_to_all x5 -> x0, starting transfers between devices: 26.7 us -> none  [the longest x2 9.24 us: ffn_tp(): back = lax.all_to_all(pr.reshape(-1, b, pr.shape[1]), 'tp', 0, 0)]
    unnamed x14 -> x3, local copies, waits for them, and re-layouts: 0.03 us -> 10.1 us
    all_to_all x5 -> x0, waiting for transfers between devices: 10 us -> none  [the longest x1 9.63 us: moe_ep(): lax.all_to_all(out.reshape(n, cap, h), GROUP, 0, 0).reshape(n * cap, h)]
  transfers between devices with their start and end apart: 5 -> 0, of which waited for: 2 -> 0; matrix products, arithmetic and copies ran while one was open for 54% -> 0% of each run, Pallas kernels for 17% -> 0%
where the time goes in v1:
time: 84.3 us; the launch traced here: 83.9 us
  Pallas kernels  73.8 us (88%)
  local copies, waits for them, and re-layouts  10.1 us (12%)
    pallas_call x1, Pallas kernels, layer(): pl.pallas_call(functools.partial(kernel, tuple(sc)), out_shape=jax.ShapeD...  73.8 us
    unnamed x3, local copies, waits for them, and re-layouts  10.1 us

profile of v1, /device:TPU:0, one launch (start us, length us, event | category | flops | bytes accessed | tf_op | source)
XLA Modules:
  0.0 83.9 jit_solution(6195406568136228531)
XLA Ops:
  0.0 4.3 %copy.16.kv0 = bf16[8,256,576]{2,1,0:T(8,128)(2,1)} copy(bf16[8,256,576]{1,2,0:T(8,128)(2,1)} %param.16) | data formatting | bytes 4718592 | tf_op args[1]
  4.3 4.4 %copy.17.kv1 = bf16[8,256,576]{2,1,0:T(8,128)(2,1)} copy(bf16[8,256,576]{1,2,0:T(8,128)(2,1)} %param.17) | data formatting | bytes 4718592 | tf_op args[2]
  8.7 73.8 %shard_map.145 = bf16[8,2048]{1,0:T(8,128)(2,1)} custom-call(bf16[8,2048]{1,0:T(8,128)(2,1)} %x.1, s32[8]{0:T(128)} %lens.1, s32[8,6]{1,0:T(8,128)} %ids.1, f32[8,6]{1,0:T(8,128)} %wts.1, bf16[256,384]{1,0:T(8,128)(2,1)} %constant.2.clone.table, bf16[8,256,576]{2,1,0:T(8,128)(2,1)} %copy.16.kv0, bf16[8,256,576]{2,1,0:T(8,128)(2,1)} %copy.17.kv1, ...), custom_call_target="tpu_custom_call" | custom-call | tf_op jit(solution)/shard_map/pallas_call | solution.py:484
  82.5 1.4 %copy.19 = bf16[8,2048]{1,0:T(8,128)(2,1)} copy(bf16[8,2048]{1,0:T(8,128)(2,1)} %shard_map.145) | data formatting | bytes 65536

commit v2 on v1

--- a/solution.py
+++ b/solution.py
@@ -39,9 +39,9 @@
     dma = pltpu.SemaphoreType.DMA
     v = pltpu.VMEM
     return dict(
-        mbuf=v((8, H, CB), BF), wukb=v((HEADS, NOPE, LAT), BF), wuvb=v((HEADS, LAT, VH), BF), kvb=v((B * L, LAT + ROPE), BF),
+        mbuf=v((8, H, CB), BF), wukb=v((HEADS, NOPE, LAT), BF), wuvb=v((HEADS, LAT, VH), BF), kvb=v((B, LAT + ROPE, L), BF),
         gu5=v((2, 5, H, CB), BF), gu1=v((2, H, CB // 2), BF), wd=v((2, 4, FH, CB), BF),
-        qs=v((B, HEADS * (NOPE + ROPE)), F32), qc=v((R, LAT + ROPE), BF), sc=v((R, L), F32), pb=v((R, B * L), BF),
+        qs=v((B, HEADS * (NOPE + ROPE)), F32), qc=v((R, LAT + ROPE), BF), sc=v((R, L), F32),
         ol=v((R, LAT), F32), os=v((B, HEADS * VH), BF), res=v((B, H), F32), an=v((B, H), BF),
         h0=v((B, H), BF), f0=v((B, H), BF), h1=v((B, H), BF),
         cs=v((R, ROPE), F32), sn=v((R, ROPE), F32), lm=v((R, L), F32),
@@ -98,7 +98,7 @@
         return cp(wo.at[l, :, pl.ds(j * CB, CB)], s.mbuf.at[k], s.s_m.at[k])
 
     def c_kv(l, t):
-        return cp(kvs[l].at[t], s.kvb.at[pl.ds(t * L, L)], s.s_kv.at[t])
+        return cp(kvs[l].at[t], s.kvb.at[t], s.s_kv.at[t])
 
     def c_uk(l):
         return cp(wuk.at[l], s.wukb, s.s_uk.at[0])
@@ -198,7 +198,7 @@
         s.qc[:, LAT:] = (r * s.cs[...] + rot * s.sn[...]).astype(BF)
         for t in range(B):
             c_kv(l, t).wait()
-            st = lax.dot_general(s.qc[...], s.kvb[t * L:(t + 1) * L, :], (((1,), (1,)), ((), ())), preferred_element_type=F32)
+            st = dot(s.qc[...], s.kvb[t])
             if t == 0:
                 s.sc[...] = st
             else:
@@ -206,9 +206,12 @@
         sc = jnp.where(lax.broadcasted_iota(I32, (R, L), 1).astype(F32) < s.lm[...], s.sc[...] * SCALE, -1e30)
         ex = jnp.exp(sc - jnp.max(sc, axis=-1, keepdims=True))
         p = ex / jnp.sum(ex, axis=-1, keepdims=True)
+        ol = None
         for t in range(B):
-            s.pb[:, t * L:(t + 1) * L] = jnp.where(rowt == t, p, 0.0).astype(BF)
-        s.ol[...] = dot(s.pb[...], s.kvb[:, :LAT])
+            pt = jnp.where(rowt == t, p, 0.0).astype(BF)
+            ot = lax.dot_general(pt, s.kvb[t, :LAT, :], (((1,), (1,)), ((), ())), preferred_element_type=F32)
+            ol = ot if ol is None else ol + ot
+        s.ol[...] = ol
         after_kv()
         c_uv(l).wait()
         for h in range(HEADS):
@@ -488,7 +491,7 @@
         out_specs=vm,
         scratch_shapes=list(sc.values()),
         compiler_params=pltpu.CompilerParams(collective_id=0, has_side_effects=True, vmem_limit_bytes=67043328),
-    )(x, lens, ids, wts, table, kv0, kv1, wq, wuk, wuv, wo, w_in, w_out, e_in, e_out)
+    )(x, lens, ids, wts, table, jnp.swapaxes(kv0, 1, 2), jnp.swapaxes(kv1, 1, 2), wq, wuk, wuv, wo, w_in, w_out, e_in, e_out)
 
 
 def solution(mesh):

time: 84.3 us -> 75.3 us (0.89)
  local copies, waits for them, and re-layouts: 10.1 us -> 1.38 us
    unnamed x3 -> x1, local copies, waits for them, and re-layouts: 10.1 us -> 1.38 us
where the time goes in v2:
time: 75.3 us; the launch traced here: 75.1 us
  Pallas kernels  73.7 us (98%)
  local copies, waits for them, and re-layouts  1.38 us (2%)
    pallas_call x1, Pallas kernels, layer(): pl.pallas_call(functools.partial(kernel, tuple(sc)), out_shape=jax.ShapeD...  73.7 us

profile of v2, /device:TPU:0, one launch (start us, length us, event | category | flops | bytes accessed | tf_op | source)
XLA Modules:
  0.0 75.1 jit_solution(6367297436003364937)
XLA Ops:
  0.0 73.7 %shard_map.145 = bf16[8,2048]{1,0:T(8,128)(2,1)} custom-call(bf16[8,2048]{1,0:T(8,128)(2,1)} %x.1, s32[8]{0:T(128)} %lens.1, s32[8,6]{1,0:T(8,128)} %ids.1, f32[8,6]{1,0:T(8,128)} %wts.1, bf16[256,384]{1,0:T(8,128)(2,1)} %constant.2.clone.table, bf16[8,576,256]{2,1,0:T(8,128)(2,1)} %bitcast.2, bf16[8,576,256]{2,1,0:T(8,128)(2,1)} %bitcast.3, ...), custom_call_target="tpu_custom_call" | custom-call | tf_op jit(solution)/shard_map/pallas_call | solution.py:487
  73.7 1.4 %copy.17 = bf16[8,2048]{1,0:T(8,128)(2,1)} copy(bf16[8,2048]{1,0:T(8,128)(2,1)} %shard_map.145) | data formatting | bytes 65536
